TPU v7x, 32 devices: a whole 2x2x4 slice. The times are simulated.
32 devices in a mesh: grp: 2 (over core), dp: 4 (over z), seq: 4 (over y, x).
Axes of the slice: x: 2, y: 2, z: 4, core: 2. Of those that a mesh axis runs over, the one named last changes fastest.
Arguments:
- latents: bfloat16 [4, 512, 3072], P('dp', 'seq'), may hold values from -6 to 6
- attended: bfloat16 [4, 512, 1536], P('dp', 'seq'), may hold values from -6 to 6
- gating: float32 [4, 3072], P('dp'), may hold values from -4 to 4
- weights: bfloat16 [2, 3072, 1536], P('grp', ('dp', 'seq')), may hold values from -0.15625 to 0.15625
- critic_position: bfloat16 [512, 3072], P('seq'), may hold values from -6 to 6
- critic_gain: float32 [3072], replicated, may hold values from 0.1 to 1.9
- critic_head: float32 [1536], replicated, may hold values from -0.15625 to 0.15625
- token_order: int32 [512], replicated, may hold values from 0 to 511, as said below
Outputs:
- weight_grads: float32 [2, 3072, 1536], P('grp', ('dp', 'seq'))
Inputs may be any that keep to these rules, and one draw needn't show every extreme that they name: token_order is a permutation of the 512 positions; of each aligned block of 128 entries, exactly 32 values fall in each aligned block of 128 values.
All inputs are finite; a program needn't handle non-finite values.
Results may differ from a plain program's by a relative error of at most 0.0029.
Values may be sent and summed in bfloat16 or wider, within the bound.
No kernel may reach another device: no remote copies, remote signals or barrier semaphores. Data moves between devices by JAX's collectives and lax.ppermute only.
A program may use at most 64 MiB of HBM per device.

v0:
```python
from functools import partial
import jax
import jax.numpy as jnp
from jax import lax
from jax.sharding import PartitionSpec as P


def from_behind(block, axis, distance):
    devices = range(lax.axis_size(axis))
    route = [(i - distance, i) for i in devices if i - distance in devices]
    return lax.ppermute(block, axis, route)


def normalize(values, gain):
    factor = lax.rsqrt(jnp.mean(values * values, axis=-1, keepdims=True) + 1e-06)
    return values * factor * gain


def critic_score(hidden, head):
    return jnp.sum(jax.nn.gelu(hidden, approximate=True) * head, axis=-1)


def shards(
    latents, attended, gating, weights, critic_position, critic_gain, critic_head, token_order
):
    length = latents.shape[1]
    model_width = latents.shape[2]
    feature_width = attended.shape[2]
    seq_count = lax.axis_size("seq")
    share_count = length // seq_count
    is_maker = lax.axis_index("grp") == 0
    seq_place = lax.axis_index("seq")
    full_weight = lax.all_gather(weights[0], ("dp", "seq"), axis=0, tiled=True)

    def make_fake():
        projected = jnp.einsum(
            "th,dh->td", attended[0], full_weight, preferred_element_type=jnp.float32
        )
        return (latents[0].astype(jnp.float32) + gating[0][None, :] * projected).astype(
            jnp.bfloat16
        )

    def skip_fake():
        return jnp.zeros((length, model_width), jnp.bfloat16)

    fake_clip = lax.cond(is_maker, make_fake, skip_fake)
    blocks = token_order.reshape(seq_count, length)
    sources = blocks // length
    offsets = jnp.arange(length, dtype=jnp.int32)
    sort_keys = jnp.where(sources == seq_place, offsets[None, :], length + offsets[None, :])
    picked = jnp.argsort(sort_keys, axis=1)[:, :share_count]
    send_rows = (jnp.take_along_axis(blocks, picked, axis=1) - seq_place * length).reshape(-1)
    own_block = lax.dynamic_index_in_dim(blocks, seq_place, 0, keepdims=False)
    own_source = own_block // length
    indicator = (own_source[:, None] == jnp.arange(seq_count, dtype=jnp.int32)[None, :]).astype(
        jnp.int32
    )
    rank_in = jnp.sum(jnp.cumsum(indicator, axis=0) * indicator, axis=1) - 1
    recv_rows = own_source * share_count + rank_in
    outgoing = fake_clip[send_rows].reshape(seq_count, share_count, model_width)
    crossed = from_behind(outgoing, "grp", 1)
    arrived = lax.all_to_all(crossed, "seq", split_axis=0, concat_axis=0, tiled=True)
    critic_tokens = arrived.reshape(length, model_width)[recv_rows]

    def run_critic():
        critic_in = critic_tokens.astype(jnp.float32) + critic_position.astype(jnp.float32)
        normed, norm_back = jax.vjp(partial(normalize, gain=critic_gain), critic_in)
        normed_b = normed.astype(jnp.bfloat16)
        hidden = jnp.dot(normed_b, full_weight, preferred_element_type=jnp.float32)
        scores, score_back = jax.vjp(partial(critic_score, head=critic_head), hidden)
        hidden_grad = score_back(-jax.nn.sigmoid(-scores))[0].astype(jnp.bfloat16)
        normed_grad = jnp.einsum(
            "th,dh->td", hidden_grad, full_weight, preferred_element_type=jnp.float32
        )
        input_grad = norm_back(normed_grad)[0].astype(jnp.bfloat16)
        return (normed_b, hidden_grad, input_grad)

    def skip_critic():
        return (
            jnp.zeros((length, model_width), jnp.bfloat16),
            jnp.zeros((length, feature_width), jnp.bfloat16),
            jnp.zeros((length, model_width), jnp.bfloat16),
        )

    normed_b, hidden_grad, input_grad = lax.cond(jnp.logical_not(is_maker), run_critic, skip_critic)
    returning = input_grad[jnp.argsort(recv_rows)].reshape(seq_count, share_count, model_width)
    regrouped = lax.all_to_all(returning, "seq", split_axis=0, concat_axis=0, tiled=True)
    returned = from_behind(regrouped, "grp", -1)
    fake_grad = returned.reshape(length, model_width)[jnp.argsort(send_rows)]
    projected_grad = (gating[0][None, :] * fake_grad.astype(jnp.float32)).astype(jnp.bfloat16)
    left_side = jnp.where(is_maker, projected_grad, normed_b)
    right_side = jnp.where(is_maker, attended[0], hidden_grad)
    summed = lax.psum_scatter(
        jnp.einsum("td,th->dh", left_side, right_side, preferred_element_type=jnp.float32),
        ("dp", "seq"),
        scatter_dimension=0,
        tiled=True,
    )
    return summed[None]


def solution(mesh):
    return jax.shard_map(
        shards,
        mesh=mesh,
        in_specs=(
            P("dp", "seq", None),
            P("dp", "seq", None),
            P("dp", None),
            P("grp", ("dp", "seq"), None),
            P("seq", None),
            P(),
            P(),
            P(),
        ),
        out_specs=P("grp", ("dp", "seq"), None),
        check_vma=False,
    )
```

profile of v0, /device:TPU:0, one launch (start us, length us, event | category | flops | bytes accessed | tf_op | source)
XLA Modules:
  0.0 489.7 jit_solution(7925361353231627886)
XLA Ops:
  7.4 1.4 iota_select_fusion
  8.8 0.6 iota.26
  9.5 0.5 all-gather.3.cloned.1.call-update
  10.0 3.0 sort.52.cloned.1.call-done
  13.0 0.7 bitcast_or_fusion
  13.8 1.5 gather_fusion.4
  15.5 121.5 %all-gather.3.cloned.1.call-done = bf16[1,3072,1536]{2,1,0:T(8,128)(2,1)} async-done(((bf16[1,192,1536]{2,1,0:T(8,128)(2,1)}), bf16[1,3072,1536]{2,1,0:T(8,128)(2,1)}) %all-gather.3.cloned.1.call-update) | async-done | bytes 9437200 | tf_op jit(solution)/shard_map/all_gather | solution.py:33
  137.0 6.9 %conditional.2 = (bf16[128,3072]{1,0:T(8,128)(2,1)S(1)}) conditional(s32[]{:T(128)} %convert_element_type.45, () %tuple.23, (bf16[1,128,3072]{2,1,0:T(8,128)(2,1)S(1)}, f32[1,3072]{1,0:T(1,128)S(1)}, bf16[1,128,1536]{2,1,0:T(8,128)(2,1)S(1)}, bf16[3072,1536]{1,0:T(8,128)(2,1)}) %tuple.49), branch_computations={%region_0.0_spmd, %region_1.0_spmd} | conditional | flops 1209532416 | bytes 11415560 | solution.py:46
  137.1 6.8 %fusion.1 = bf16[128,3072]{1,0:T(8,128)(2,1)S(1)} fusion(bf16[3072,1536]{1,0:T(8,128)(2,1)} %get-tuple-element.117, bf16[1,128,3072]{2,1,0:T(8,128)(2,1)S(1)} %get-tuple-element.141, f32[3072]{0:T(1024)S(1)} %bitcast.64, bf16[1,128,1536]{2,1,0:T(8,128)(2,1)S(1)} %get-tuple-element.116), kind=kOutput, calls=%fused_computation.7 | convolution fusion | flops 1209532416 | bytes 11415552 | tf_op jit(solution)/shard_map/cond/branch_1_fun/th,dh->td/dot_general | solution.py:36
  143.9 1.0 gather_fusion.1
  144.9 2.3 collective-permute-start
  147.7 0.7 collective-permute-done
  148.4 3.5 all-to-all-start
  152.0 2.5 sort.49
  154.6 9.0 %all-to-all-done = bf16[4,32,3072]{2,1,0:T(8,128)(2,1)S(1)} async-done(((bf16[4,32,3072]{2,1,0:T(8,128)(2,1)}), bf16[4,32,3072]{2,1,0:T(8,128)(2,1)S(1)}, u32[]{:S(2)}, u32[]{:S(2)}) %all-to-all-start) | async-done | bytes 786464 | tf_op jit(solution)/shard_map/all_to_all | solution.py:62
  163.5 0.2 conditional.3
  163.7 1.0 gather_fusion.2
  164.8 11.1 %all_to_all.10 = bf16[4,32,3072]{2,1,0:T(8,128)(2,1)S(1)} all-to-all(bf16[4,32,3072]{2,1,0:T(8,128)(2,1)S(1)} %bitcast.61), channel_id=1, replica_groups=mesh['grp'=2,'dp'=4,'seq'=4] {'seq'}, dimensions={0} | all-to-all | bytes 1572864 | tf_op jit(solution)/shard_map/all_to_all | solution.py:87
  175.8 1.3 collective-permute-start.1
  177.2 2.5 sort.50
  179.8 10.4 %collective-permute-done.1 = bf16[4,32,3072]{2,1,0:T(8,128)(2,1)S(1)} collective-permute-done((bf16[4,32,3072]{2,1,0:T(8,128)(2,1)S(1)}, bf16[4,32,3072]{2,1,0:T(8,128)(2,1)S(1)}, u32[]{:S(2)}, u32[]{:S(2)}) %collective-permute-start.1) | collective-permute-done | bytes 786464 | tf_op jit(solution)/shard_map/ppermute | solution.py:11
  190.2 1.0 gather_fusion.3
  191.2 7.9 %fusion.17 = f32[3072,1536]{1,0:T(8,128)} fusion(bf16[128,3072]{1,0:T(8,128)(2,1)S(1)} %get-tuple-element.138, bf16[128,3072]{1,0:T(8,128)(2,1)S(1)} %gather_fusion.3, f32[3072]{0:T(1024)S(1)} %bitcast.63, pred[]{:T(512)S(6)} %eq.22, bf16[128,1536]{1,0:T(8,128)(2,1)S(1)} %get-tuple-element.139, bf16[1,128,1536]{2,1,0:T(8,128)(2,1)S(1)} %copy-done.7), kind=kOutput, calls=%fused_computation.45 | convolution fusion | flops 1209729024 | bytes 21245952 | tf_op jit(solution)/shard_map/td,th->dh/dot_general | solution.py:94
  199.2 283.1 %reduce-scatter.2.cloned.1.call-done = f32[192,1536]{1,0:T(8,128)} async-done(((f32[3072,1536]{1,0:T(8,128)}), f32[192,1536]{1,0:T(8,128)}) %reduce-scatter.2.cloned.1.call-update) | async-done | bytes 1179664 | tf_op jit(solution)/shard_map/reduce_scatter | solution.py:93
  (46 shorter events, 1.2 us)
Async XLA Ops:
  7.4 6.4 %copy-start = (s32[512]{0:T(512)S(1)}, s32[512]{0:T(512)}, u32[]{:S(2)}) copy-start(s32[512]{0:T(512)} %param.19) | copy-start | bytes 6148
  7.4 129.6 %copy-start.9 = (f32[1,3072]{1,0:T(1,128)S(1)}, f32[1,3072]{1,0:T(1,128)}, u32[]{:S(2)}) copy-start(f32[1,3072]{1,0:T(1,128)} %param.14) | copy-start | bytes 36868
  7.4 129.6 %copy-start.6 = (bf16[1,128,1536]{2,1,0:T(8,128)(2,1)S(1)}, bf16[1,128,1536]{2,1,0:T(8,128)(2,1)}, u32[]{:S(2)}) copy-start(bf16[1,128,1536]{2,1,0:T(8,128)(2,1)} %param.13) | copy-start | bytes 1179652
  7.4 129.6 %copy-start.8 = (bf16[1,128,3072]{2,1,0:T(8,128)(2,1)S(1)}, bf16[1,128,3072]{2,1,0:T(8,128)(2,1)}, u32[]{:S(2)}) copy-start(bf16[1,128,3072]{2,1,0:T(8,128)(2,1)} %param.12) | copy-start | bytes 2359300
  7.4 5.6 %sort.52.cloned.1.call-start = ((), (), s32[]{:S(2)}) async-start(), calls=%async_computation.5 | async-start | bytes 12320 | tf_op jit(solution)/shard_map/jit(argsort)/sort | solution.py:51
  9.4 127.6 %all-gather.3.cloned.1.call-start = ((), (), s32[]{:S(2)}) async-start(), calls=%async_computation.4 | async-start | bytes 10027008 | tf_op jit(solution)/shard_map/all_gather | solution.py:33
  13.0 2.4 copy-start.14
  15.4 121.6 %copy-start.11 = (s32[4,32]{1,0:T(4,128)}, s32[4,32]{1,0:T(4,128)S(1)}, u32[]{:S(2)}) copy-start(s32[4,32]{1,0:T(4,128)S(1)} %select_subtract_fusion) | copy-start | bytes 1540
  144.9 18.6 %copy-start.1 = (bf16[128,3072]{1,0:T(8,128)(2,1)S(1)}, bf16[128,3072]{1,0:T(8,128)(2,1)}, u32[]{:S(2)}) copy-start(bf16[128,3072]{1,0:T(8,128)(2,1)} %param.16) | copy-start | bytes 2359300
  144.9 3.5 collective-permute-start
  148.4 15.1 %all-to-all-start = ((bf16[4,32,3072]{2,1,0:T(8,128)(2,1)}), bf16[4,32,3072]{2,1,0:T(8,128)(2,1)S(1)}, u32[]{:S(2)}, u32[]{:S(2)}) async-start(bf16[4,32,3072]{2,1,0:T(8,128)(2,1)} %collective-permute-done), calls=%async_computation | async-start | bytes 1572864 | tf_op jit(solution)/shard_map/all_to_all | solution.py:62
  151.9 330.4 %reduce-scatter.2.cloned.1.call-start = ((), (), s32[]{:S(2)}) async-start(), calls=%async_computation.3 | async-start | bytes 20054016 | tf_op jit(solution)/shard_map/reduce_scatter | solution.py:93
  164.8 12.4 %copy-start.12 = (s32[4,32]{1,0:T(4,128)S(1)}, s32[4,32]{1,0:T(4,128)}, u32[]{:S(2)}) copy-start(s32[4,32]{1,0:T(4,128)} %copy-done.11) | copy-start | bytes 1540
  175.8 14.3 %collective-permute-start.1 = (bf16[4,32,3072]{2,1,0:T(8,128)(2,1)S(1)}, bf16[4,32,3072]{2,1,0:T(8,128)(2,1)S(1)}, u32[]{:S(2)}, u32[]{:S(2)}) collective-permute-start(bf16[4,32,3072]{2,1,0:T(8,128)(2,1)S(1)} %all_to_all.10), channel_id=1, source_target_pairs={{16,0},{17,1},{18,2},{19,3},{20,4},{21,5},{22,6},{23,7},{24,8},{25... | collective-permute-start | bytes 2359304 | tf_op jit(solution)/shard_map/ppermute | solution.py:11
  190.2 1.0 copy-start.7
Sparse Core Ops, SparseCore 0:
  10.4 2.2 sort.54.cloned.1.call-done
  (1 shorter events, 0.0 us)
Sparse Core Ops, SparseCore 1:
  12.7 124.3 all-gather.2
  199.2 283.0 reduce-scatter.1
where the time goes:
time: 490 us
  waiting for transfers between devices  425 us (87%)
  between operations  15 us (3%)
  matrix products  14.7 us (3%)
  blocking collectives  11.1 us (2%)
  local copies, waits for them, and re-layouts  8.77 us (2%)
  other arithmetic  7.69 us (2%)
  starting transfers between devices  7.17 us (1%)
    reduce_scatter x1, waiting for transfers between devices, shards(): lax.psum_scatter(jnp.einsum('td,th->dh', left_side, right_side, preferred...  283 us
    all_gather x1, waiting for transfers between devices, shards(): full_weight = lax.all_gather(weights[0], ('dp', 'seq'), axis=0, tiled=True)  121 us
    ppermute x2, waiting for transfers between devices, from_behind(): return lax.ppermute(block, axis, route)  11.1 us
    all_to_all x1, blocking collectives, shards(): lax.all_to_all(returning, 'seq', split_axis=0, concat_axis=0, tiled=True)  11.1 us
  transfers between devices with their start and end apart: 5, of which 5 were waited for; matrix products, arithmetic and copies ran while one was open for 2% of the time, Pallas kernels for 0%

commit v1 on v0

--- a/solution.py
+++ b/solution.py
@@ -30,7 +30,10 @@
     share_count = length // seq_count
     is_maker = lax.axis_index("grp") == 0
     seq_place = lax.axis_index("seq")
-    full_weight = lax.all_gather(weights[0], ("dp", "seq"), axis=0, tiled=True)
+    full_weight = jnp.concatenate(
+        lax.all_to_all(jnp.stack([weights[0]] * lax.axis_size(("dp", "seq"))), ("dp", "seq"), 0, 0),
+        axis=0,
+    )
 
     def make_fake():
         projected = jnp.einsum(

time: 490 us -> 594 us (1.21)
  waiting for transfers between devices: 425 us -> 503 us
  starting transfers between devices: 7.17 us -> 27 us
  local copies, waits for them, and re-layouts: 8.77 us -> 15.9 us
    all_to_all x0 -> x1, waiting for transfers between devices: none -> 170 us  [shards(): lax.all_to_all(jnp.stack([weights[0]] * lax.axis_size(('dp', 'seq'))), ('...]
    all_gather x1 -> x0, waiting for transfers between devices: 121 us -> none  [shards(): full_weight = lax.all_gather(weights[0], ('dp', 'seq'), axis=0, tiled=True)]
    reduce_scatter x1, waiting for transfers between devices: 283 us -> 310 us  [shards(): lax.psum_scatter(jnp.einsum('td,th->dh', left_side, right_side, preferred...]
    all_to_all x1, starting transfers between devices: 3.49 us -> 14.9 us  [shards(): lax.all_to_all(crossed, 'seq', split_axis=0, concat_axis=0, tiled=True)]
    all_to_all x0 -> x1, starting transfers between devices: none -> 8.52 us  [shards(): lax.all_to_all(jnp.stack([weights[0]] * lax.axis_size(('dp', 'seq'))), ('...]
where the time goes in v1:
time: 594 us; the launch traced here: 593 us
  waiting for transfers between devices  503 us (85%)
  starting transfers between devices  27 us (5%)
  local copies, waits for them, and re-layouts  15.9 us (3%)
  matrix products  14.8 us (2%)
  between operations  13.6 us (2%)
  blocking collectives  11 us (2%)
  other arithmetic  7.51 us (1%)
    reduce_scatter x1, waiting for transfers between devices, shards(): lax.psum_scatter(jnp.einsum('td,th->dh', left_side, right_side, preferred...  310 us
    all_to_all x1, waiting for transfers between devices, shards(): lax.all_to_all(jnp.stack([weights[0]] * lax.axis_size(('dp', 'seq'))), ('...  170 us
    all_to_all x1, starting transfers between devices, shards(): lax.all_to_all(crossed, 'seq', split_axis=0, concat_axis=0, tiled=True)  14.9 us
    ppermute x2, waiting for transfers between devices, from_behind(): return lax.ppermute(block, axis, route)  14.7 us
  transfers between devices with their start and end apart: 5, of which 5 were waited for; matrix products, arithmetic and copies ran while one was open for 2% of the time, Pallas kernels for 0%

profile of v1, /device:TPU:0, one launch (start us, length us, event | category | flops | bytes accessed | tf_op | source)
XLA Modules:
  0.0 593.0 jit_solution(13529353357310603598)
XLA Ops:
  6.5 5.6 stack.3
  12.2 8.5 %all-to-all-start = ((bf16[16,192,1536]{2,1,0:T(8,128)(2,1)}), bf16[16,192,1536]{2,1,0:T(8,128)(2,1)}, u32[]{:S(2)}, u32[]{:S(2)}) async-start(bf16[16,192,1536]{2,1,0:T(8,128)(2,1)} %stack.3), calls=%async_computation | async-start | bytes 18874368 | tf_op jit(solution)/shard_map/all_to_all | solution.py:34
  20.8 0.6 iota_select_fusion
  22.0 4.3 sort.52.cloned.1.call-done
  26.4 0.8 bitcast_or_fusion
  27.2 1.5 gather_fusion.4
  28.9 169.7 %all-to-all-done = bf16[16,192,1536]{2,1,0:T(8,128)(2,1)} async-done(((bf16[16,192,1536]{2,1,0:T(8,128)(2,1)}), bf16[16,192,1536]{2,1,0:T(8,128)(2,1)}, u32[]{:S(2)}, u32[]{:S(2)}) %all-to-all-start) | async-done | bytes 9437216 | tf_op jit(solution)/shard_map/all_to_all | solution.py:34
  198.7 6.9 %conditional.2 = (bf16[128,3072]{1,0:T(8,128)(2,1)S(1)}) conditional(s32[]{:T(128)} %convert_element_type.45, () %tuple.23, (bf16[1,128,3072]{2,1,0:T(8,128)(2,1)S(1)}, f32[1,3072]{1,0:T(1,128)S(1)}, bf16[1,128,1536]{2,1,0:T(8,128)(2,1)S(1)}, bf16[3072,1536]{1,0:T(8,128)(2,1)}) %tuple.45), branch_computations={%region_0.0_spmd, %region_1.0_spmd} | conditional | flops 1209532416 | bytes 11415560 | solution.py:49
  198.7 6.8 %fusion.1 = bf16[128,3072]{1,0:T(8,128)(2,1)S(1)} fusion(bf16[3072,1536]{1,0:T(8,128)(2,1)} %get-tuple-element.117, bf16[1,128,3072]{2,1,0:T(8,128)(2,1)S(1)} %get-tuple-element.141, f32[3072]{0:T(1024)S(1)} %bitcast.62, bf16[1,128,1536]{2,1,0:T(8,128)(2,1)S(1)} %get-tuple-element.116), kind=kOutput, calls=%fused_computation.7 | convolution fusion | flops 1209532416 | bytes 11415552 | tf_op jit(solution)/shard_map/cond/branch_1_fun/th,dh->td/dot_general | solution.py:39
  205.5 1.0 gather_fusion.1
  206.6 2.3 collective-permute-start
  209.4 0.7 collective-permute-done
  210.1 14.9 %all-to-all-start.1 = ((bf16[4,32,3072]{2,1,0:T(8,128)(2,1)}), bf16[4,32,3072]{2,1,0:T(8,128)(2,1)S(1)}, u32[]{:S(2)}, u32[]{:S(2)}) async-start(bf16[4,32,3072]{2,1,0:T(8,128)(2,1)} %collective-permute-done), calls=%async_computation.1 | async-start | bytes 1572864 | tf_op jit(solution)/shard_map/all_to_all | solution.py:65
  224.9 2.5 sort.49
  227.5 0.6 pad_clamp_fusion.2
  228.1 8.5 %all-to-all-done.1 = bf16[4,32,3072]{2,1,0:T(8,128)(2,1)S(1)} async-done(((bf16[4,32,3072]{2,1,0:T(8,128)(2,1)}), bf16[4,32,3072]{2,1,0:T(8,128)(2,1)S(1)}, u32[]{:S(2)}, u32[]{:S(2)}) %all-to-all-start.1) | async-done | bytes 786464 | tf_op jit(solution)/shard_map/all_to_all | solution.py:65
  236.7 1.2 gather_fusion.2
  237.9 11.0 %all_to_all.15 = bf16[4,32,3072]{2,1,0:T(8,128)(2,1)S(1)} all-to-all(bf16[4,32,3072]{2,1,0:T(8,128)(2,1)S(1)} %bitcast.58), channel_id=1, replica_groups=mesh['grp'=2,'dp'=4,'seq'=4] {'seq'}, dimensions={0} | all-to-all | bytes 1572864 | tf_op jit(solution)/shard_map/all_to_all | solution.py:90
  249.0 1.3 collective-permute-start.1
  250.4 2.5 sort.50
  252.9 14.1 %collective-permute-done.1 = bf16[4,32,3072]{2,1,0:T(8,128)(2,1)S(1)} collective-permute-done((bf16[4,32,3072]{2,1,0:T(8,128)(2,1)S(1)}, bf16[4,32,3072]{2,1,0:T(8,128)(2,1)S(1)}, u32[]{:S(2)}, u32[]{:S(2)}) %collective-permute-start.1) | collective-permute-done | bytes 786464 | tf_op jit(solution)/shard_map/ppermute | solution.py:11
  267.0 1.0 gather_fusion.3
  268.0 7.9 %fusion.17 = f32[3072,1536]{1,0:T(8,128)} fusion(bf16[128,3072]{1,0:T(8,128)(2,1)S(1)} %get-tuple-element.138, bf16[128,3072]{1,0:T(8,128)(2,1)S(1)} %gather_fusion.3, f32[3072]{0:T(1024)S(1)} %bitcast.61, pred[]{:T(512)S(6)} %eq.22, bf16[128,1536]{1,0:T(8,128)(2,1)S(1)} %get-tuple-element.139, bf16[1,128,1536]{2,1,0:T(8,128)(2,1)S(1)} %copy-done.7), kind=kOutput, calls=%fused_computation.45 | convolution fusion | flops 1209729024 | bytes 21245952 | tf_op jit(solution)/shard_map/td,th->dh/dot_general | solution.py:97
  276.0 310.2 %reduce-scatter.2.cloned.1.call-done = f32[192,1536]{1,0:T(8,128)} async-done(((f32[3072,1536]{1,0:T(8,128)}), f32[192,1536]{1,0:T(8,128)}) %reduce-scatter.2.cloned.1.call-update) | async-done | bytes 1179664 | tf_op jit(solution)/shard_map/reduce_scatter | solution.py:96
  (46 shorter events, 1.9 us)
Async XLA Ops:
  12.2 8.6 %copy-start = (s32[512]{0:T(512)S(1)}, s32[512]{0:T(512)}, u32[]{:S(2)}) copy-start(s32[512]{0:T(512)} %param.19) | copy-start | bytes 6148
  12.2 186.5 %all-to-all-start = ((bf16[16,192,1536]{2,1,0:T(8,128)(2,1)}), bf16[16,192,1536]{2,1,0:T(8,128)(2,1)}, u32[]{:S(2)}, u32[]{:S(2)}) async-start(bf16[16,192,1536]{2,1,0:T(8,128)(2,1)} %stack.3), calls=%async_computation | async-start | bytes 18874368 | tf_op jit(solution)/shard_map/all_to_all | solution.py:34
  20.7 178.0 %copy-start.6 = (bf16[1,128,1536]{2,1,0:T(8,128)(2,1)S(1)}, bf16[1,128,1536]{2,1,0:T(8,128)(2,1)}, u32[]{:S(2)}) copy-start(bf16[1,128,1536]{2,1,0:T(8,128)(2,1)} %param.13) | copy-start | bytes 1179652
  20.7 177.9 %copy-start.8 = (bf16[1,128,3072]{2,1,0:T(8,128)(2,1)S(1)}, bf16[1,128,3072]{2,1,0:T(8,128)(2,1)}, u32[]{:S(2)}) copy-start(bf16[1,128,3072]{2,1,0:T(8,128)(2,1)} %param.12) | copy-start | bytes 2359300
  20.7 177.9 %copy-start.9 = (f32[1,3072]{1,0:T(1,128)S(1)}, f32[1,3072]{1,0:T(1,128)}, u32[]{:S(2)}) copy-start(f32[1,3072]{1,0:T(1,128)} %param.14) | copy-start | bytes 36868
  20.7 5.6 sort.52.cloned.1.call-start
  26.4 2.4 copy-start.14
  28.8 169.9 %copy-start.11 = (s32[4,32]{1,0:T(4,128)}, s32[4,32]{1,0:T(4,128)S(1)}, u32[]{:S(2)}) copy-start(s32[4,32]{1,0:T(4,128)S(1)} %select_subtract_fusion) | copy-start | bytes 1540
  206.6 30.0 %copy-start.1 = (bf16[128,3072]{1,0:T(8,128)(2,1)S(1)}, bf16[128,3072]{1,0:T(8,128)(2,1)}, u32[]{:S(2)}) copy-start(bf16[128,3072]{1,0:T(8,128)(2,1)} %param.16) | copy-start | bytes 2359300
  206.6 3.5 collective-permute-start
  210.1 26.5 %all-to-all-start.1 = ((bf16[4,32,3072]{2,1,0:T(8,128)(2,1)}), bf16[4,32,3072]{2,1,0:T(8,128)(2,1)S(1)}, u32[]{:S(2)}, u32[]{:S(2)}) async-start(bf16[4,32,3072]{2,1,0:T(8,128)(2,1)} %collective-permute-done), calls=%async_computation.1 | async-start | bytes 1572864 | tf_op jit(solution)/shard_map/all_to_all | solution.py:65
  224.9 361.3 %reduce-scatter.2.cloned.1.call-start = ((), (), s32[]{:S(2)}) async-start(), calls=%async_computation.4 | async-start | bytes 20054016 | tf_op jit(solution)/shard_map/reduce_scatter | solution.py:96
  237.9 12.3 %copy-start.12 = (s32[4,32]{1,0:T(4,128)S(1)}, s32[4,32]{1,0:T(4,128)}, u32[]{:S(2)}) copy-start(s32[4,32]{1,0:T(4,128)} %copy-done.11) | copy-start | bytes 1540
  249.0 18.0 %collective-permute-start.1 = (bf16[4,32,3072]{2,1,0:T(8,128)(2,1)S(1)}, bf16[4,32,3072]{2,1,0:T(8,128)(2,1)S(1)}, u32[]{:S(2)}, u32[]{:S(2)}) collective-permute-start(bf16[4,32,3072]{2,1,0:T(8,128)(2,1)S(1)} %all_to_all.15), channel_id=1, source_target_pairs={{16,0},{17,1},{18,2},{19,3},{20,4},{21,5},{22,6},{23,7},{24,8},{25... | collective-permute-start | bytes 2359304 | tf_op jit(solution)/shard_map/ppermute | solution.py:11
  267.0 1.0 copy-start.7
Sparse Core Ops, SparseCore 0:
  23.8 2.2 sort.54.cloned.1.call-done
  276.1 310.0 reduce-scatter.1
  (1 shorter events, 0.0 us)
